TPU v7x, 32 devices: a whole 2x2x4 slice. The times are simulated.
32 devices in a mesh: section: 4 (over y, x), mp: 8 (over z, core).
Axes of the slice: x: 2, y: 2, z: 4, core: 2. Of those that a mesh axis runs over, the one named last changes fastest.
Arguments:
- stream: bfloat16 [512, 4096], P(('section', 'mp')), may hold values from -6 to 6
- ffn_gain: float32 [4096], replicated, may hold values from 0.25 to 1.75
- router_weight: bfloat16 [4096, 4], replicated, may hold values from -0.1875 to 0.1875
- expert_ids: int32 [512, 2], P(('section', 'mp')), may hold values from 0 to 3, all different within a row; in each aligned block of 16 rows (0 to 15, 16 to 31, ...) at most 12 rows name the same one
- w_gate: bfloat16 [4, 4096, 14336], P('section', None, 'mp'), may hold values from -0.09375 to 0.09375
- w_up: bfloat16 [4, 4096, 14336], P('section', None, 'mp'), may hold values from -0.09375 to 0.09375
- w_down: bfloat16 [4, 14336, 4096], P('section', 'mp'), may hold values from -0.09375 to 0.09375
- attn_gain: float32 [4096], replicated, may hold values from 0.25 to 1.75
- w_kv: bfloat16 [4096, 2048], P(None, 'mp'), may hold values from -0.09375 to 0.09375
Outputs:
- stream_out: bfloat16 [512, 4096], P(('section', 'mp'))
- kv_decode: bfloat16 [512, 2048], P('section', 'mp')
Inputs may be any that keep to these rules, and one draw needn't show every extreme that they name: `expert_ids`: each row names two different experts. Among the rows of one device no expert is named more than 12 times, a bound that some block reaches.
All inputs are finite; a program needn't handle non-finite values.
Results may differ from a plain program's by a relative error of at most 0.02.
Values may be sent and summed in bfloat16 or wider, within the bound.
A program may use at most 128 MiB of HBM per device.

v0:
```python
import jax
import jax.numpy as jnp
from jax import lax
from jax.sharding import PartitionSpec as P

epsilon = 1e-05


def shifted(value, axis, steps):
    count = lax.axis_size(axis)
    pairs = [(source, (source + steps) % count) for source in range(count)]
    return lax.ppermute(value, axis, pairs)


def normalize(values, scale_gain):
    floats = values.astype(jnp.float32)
    return (
        floats * lax.rsqrt(jnp.mean(floats * floats, axis=-1, keepdims=True) + epsilon) * scale_gain
    )


def body(stream, ffn_gain, router_weight, expert_ids, w_gate, w_up, w_down, attn_gain, w_kv):
    own_rows = stream.shape[0]
    model_width = stream.shape[1]
    experts = router_weight.shape[1]
    capacity = min(own_rows, 3 * own_rows // experts)
    normed = normalize(stream, ffn_gain).astype(jnp.bfloat16)
    logits = jnp.dot(normed, router_weight, preferred_element_type=jnp.float32)
    onehot = expert_ids[:, :, None] == jnp.arange(experts, dtype=jnp.int32)[None, None, :]
    chosen = jnp.sum(jnp.where(onehot, logits[:, None, :], jnp.float32(0.0)), axis=-1)
    share_first = jax.nn.sigmoid(chosen[:, 0] - chosen[:, 1])
    flat_hits = onehot.reshape(own_rows * 2, experts).astype(jnp.int32)
    before = jnp.cumsum(flat_hits, axis=0) - flat_hits
    slot_index = jnp.sum(before * flat_hits, axis=-1)
    expert_flat = expert_ids.reshape(-1)
    route_table = (
        expert_flat[None, None, :] == jnp.arange(experts, dtype=jnp.int32)[:, None, None]
    ) & (slot_index[None, None, :] == jnp.arange(capacity, dtype=jnp.int32)[None, :, None])
    route_table = route_table.astype(jnp.bfloat16)
    repeated = jnp.repeat(normed, 2, axis=0)
    buffer = jnp.einsum(
        "ecr,rd->ecd", route_table, repeated, preferred_element_type=jnp.float32
    ).astype(jnp.bfloat16)
    arrived = lax.all_to_all(buffer, "section", split_axis=0, concat_axis=0, tiled=True)
    inbound = arrived.reshape(experts * capacity, model_width)
    gate_weight = w_gate[0]
    up_weight = w_up[0]
    down_weight = w_down[0]
    block_rows = lax.all_gather(inbound, "mp", axis=0, tiled=True)
    gate_part = jnp.dot(block_rows, gate_weight, preferred_element_type=jnp.float32)
    up_part = jnp.dot(block_rows, up_weight, preferred_element_type=jnp.float32)
    hidden_all = (jax.nn.silu(gate_part) * up_part).astype(jnp.bfloat16)
    block_rows = hidden_all
    summed = lax.psum_scatter(
        jnp.dot(block_rows, down_weight, preferred_element_type=jnp.float32).astype(jnp.bfloat16),
        "mp",
        scatter_dimension=0,
        tiled=True,
    )
    results = summed.reshape(experts, capacity, model_width)
    returned = lax.all_to_all(results, "section", split_axis=0, concat_axis=0, tiled=True)
    picked = jnp.einsum("ecr,ecd->rd", route_table, returned, preferred_element_type=jnp.float32)
    picked = picked.reshape(own_rows, 2, model_width)
    updated = (
        stream.astype(jnp.float32)
        + share_first[:, None] * picked[:, 0]
        + (1.0 - share_first)[:, None] * picked[:, 1]
    )
    stream_out = updated.astype(jnp.bfloat16)
    attn_input = normalize(stream_out, attn_gain).astype(jnp.bfloat16)
    kv_local = jnp.dot(
        lax.all_gather(attn_input, "mp", axis=0, tiled=True),
        w_kv,
        preferred_element_type=jnp.float32,
    ).astype(jnp.bfloat16)
    kv_decode = shifted(kv_local, "section", 1)
    return (stream_out, kv_decode)


def solution(mesh):
    in_specs = (
        P(("section", "mp"), None),
        P(),
        P(),
        P(("section", "mp"), None),
        P("section", None, "mp"),
        P("section", None, "mp"),
        P("section", "mp", None),
        P(),
        P(None, "mp"),
    )
    out_specs = (P(("section", "mp"), None), P("section", "mp"))
    return jax.shard_map(body, mesh=mesh, in_specs=in_specs, out_specs=out_specs, check_vma=False)
```

profile of v0, /device:TPU:0, one launch (start us, length us, event | category | flops | bytes accessed | tf_op | source)
XLA Modules:
  0.0 191.3 jit_solution(9461943533034778147)
XLA Ops:
  7.2 0.0 copy-start
  7.2 0.0 all-gather.3.cloned.1.call-start
  7.2 0.9 copy.21
  8.1 0.1 eq.61
  8.2 0.1 fusion.30
  8.3 1.1 fusion.21
  9.4 0.1 reduce_window_sum.11
  9.4 0.2 select_reduce_fusion
  9.6 1.0 fusion.23
  10.6 0.2 broadcast_in_dim.16
  10.8 0.1 reshape.91
  10.9 0.3 convolution_convert_fusion
  11.2 13.5 %all_to_all.10 = bf16[4,12,4096]{2,1,0:T(8,128)(2,1)S(1)} all-to-all(bf16[4,12,4096]{2,1,0:T(8,128)(2,1)S(1)} %convolution_convert_fusion), channel_id=1, replica_groups=mesh['section'=4,'mp'=8] {'section'}, dimensions={0} | all-to-all | bytes 786432 | tf_op jit(solution)/shard_map/all_to_all | solution.py:44
  24.7 0.8 reshape.88
  25.6 0.0 all-gather.3.cloned.1.call-update
  25.6 0.0 reduce-scatter.2.cloned.1.call-start
  25.7 38.0 %all-gather.3.cloned.1.call-done = bf16[384,4096]{1,0:T(8,128)(2,1)} async-done(((bf16[48,4096]{1,0:T(8,128)(2,1)}), bf16[384,4096]{1,0:T(8,128)(2,1)}) %all-gather.3.cloned.1.call-update) | async-done | bytes 3145744 | tf_op jit(solution)/shard_map/all_gather | solution.py:49
  63.7 12.9 %fusion.4 = f32[384,1792]{1,0:T(8,128)} fusion(bf16[384,4096]{1,0:T(8,128)(2,1)} %all-gather.3.cloned.1.call-done, bf16[1,4096,1792]{2,1,0:T(8,128)(2,1)} %param.13), kind=kOutput, calls=%fused_computation.4 | convolution fusion | flops 5637144576 | bytes 20578304 | tf_op jit(solution)/shard_map/dot_general | solution.py:50
  76.6 25.0 %fusion.6 = bf16[384,4096]{1,0:T(8,128)(2,1)} fusion(bf16[1,1792,4096]{2,1,0:T(8,128)(2,1)} %param.15, bf16[384,4096]{1,0:T(8,128)(2,1)} %all-gather.3.cloned.1.call-done, bf16[1,4096,1792]{2,1,0:T(8,128)(2,1)} %param.14, f32[384,1792]{1,0:T(8,128)} %fusion.4), kind=kOutput, calls=%fused_computation.6 | convolution fusion | flops 11279990784 | bytes 38404096 | tf_op jit(solution)/shard_map/dot_general | solution.py:55
  101.6 0.0 copy-start.5
  101.6 0.0 copy-start.4
  101.6 0.0 reduce-scatter.2.cloned.1.call-update
  101.6 0.7 copy-done.5
  102.4 0.0 copy-start.1
  102.4 0.0 copy-start.3
  102.4 0.1 fusion.38
  102.5 38.6 %reduce-scatter.2.cloned.1.call-done = bf16[48,4096]{1,0:T(8,128)(2,1)} async-done(((bf16[384,4096]{1,0:T(8,128)(2,1)}), bf16[48,4096]{1,0:T(8,128)(2,1)}) %reduce-scatter.2.cloned.1.call-update) | async-done | bytes 393232 | tf_op jit(solution)/shard_map/reduce_scatter | solution.py:54
  141.1 1.9 reshape.89
  143.0 3.7 %all-to-all-start.1 = ((bf16[4,12,4096]{2,1,0:T(8,128)(2,1)}), bf16[4,12,4096]{2,1,0:T(8,128)(2,1)S(1)}, u32[]{:S(2)}, u32[]{:S(2)}) async-start(bf16[4,12,4096]{2,1,0:T(8,128)(2,1)} %reshape.89), calls=%async_computation.2 | async-start | bytes 1048576 | tf_op jit(solution)/shard_map/all_to_all | solution.py:61
  146.6 0.0 all-gather.5.cloned.1.call-start
  146.6 0.0 copy-done.4
  146.7 6.5 %all-to-all-done.1 = bf16[4,12,4096]{2,1,0:T(8,128)(2,1)S(1)} async-done(((bf16[4,12,4096]{2,1,0:T(8,128)(2,1)}), bf16[4,12,4096]{2,1,0:T(8,128)(2,1)S(1)}, u32[]{:S(2)}, u32[]{:S(2)}) %all-to-all-start.1) | async-done | bytes 393248 | tf_op jit(solution)/shard_map/all_to_all | solution.py:61
  153.2 0.3 convolution_bitcast_fusion
  153.5 0.3 reshape.90
  153.8 0.5 fusion.37
  154.4 0.0 copy-done.1
  154.4 0.4 fusion.18
  154.8 0.0 copy-start.2
  154.8 0.0 copy-done.3
  154.8 0.7 fusion.20
  155.6 0.0 all-gather.5.cloned.1.call-update
  155.6 21.7 %all-gather.5.cloned.1.call-done = bf16[128,4096]{1,0:T(8,128)(2,1)} async-done(((bf16[16,4096]{1,0:T(8,128)(2,1)}), bf16[128,4096]{1,0:T(8,128)(2,1)}) %all-gather.5.cloned.1.call-update) | async-done | bytes 1048592 | tf_op jit(solution)/shard_map/all_gather | solution.py:72
  177.2 0.0 copy-done
  177.2 1.7 convolution_convert_fusion.1
  178.9 1.5 collective-permute-start
  180.4 3.7 %collective-permute-done = bf16[128,256]{1,0:T(8,128)(2,1)S(1)} collective-permute-done((bf16[128,256]{1,0:T(8,128)(2,1)S(1)}, bf16[128,256]{1,0:T(8,128)(2,1)S(1)}, u32[]{:S(2)}, u32[]{:S(2)}) %collective-permute-start) | collective-permute-done | bytes 65568 | tf_op jit(solution)/shard_map/ppermute | solution.py:12
  184.1 0.6 copy.39
  184.8 0.0 copy-done.2
  (6 shorter events, 0.1 us)
Async XLA Ops:
  7.2 170.1 %copy-start = (bf16[4096,256]{1,0:T(8,128)(2,1)S(1)}, bf16[4096,256]{1,0:T(8,128)(2,1)}, u32[]{:S(2)}) copy-start(bf16[4096,256]{1,0:T(8,128)(2,1)} %param.17) | copy-start | bytes 6291460
  7.2 56.5 %all-gather.3.cloned.1.call-start = ((), (), s32[]{:S(2)}) async-start(), calls=%async_computation.3 | async-start | bytes 3538944 | tf_op jit(solution)/shard_map/all_gather | solution.py:49
  25.6 115.5 %reduce-scatter.2.cloned.1.call-start = ((), (), s32[]{:S(2)}) async-start(), calls=%async_computation.4 | async-start | bytes 3538944 | tf_op jit(solution)/shard_map/reduce_scatter | solution.py:54
  101.6 0.8 copy-start.5
  101.6 45.0 %copy-start.4 = (s32[16,2]{0,1:T(2,128)S(1)}, s32[16,2]{0,1:T(2,128)}, u32[]{:S(2)}) copy-start(s32[16,2]{0,1:T(2,128)} %param.12) | copy-start | bytes 388
  102.4 52.0 %copy-start.1 = (bf16[16,4096]{1,0:T(8,128)(2,1)S(1)}, bf16[16,4096]{1,0:T(8,128)(2,1)}, u32[]{:S(2)}) copy-start(bf16[16,4096]{1,0:T(8,128)(2,1)} %param.9) | copy-start | bytes 393220
  102.4 52.4 %copy-start.3 = (f32[4096]{0:T(1024)S(1)}, f32[4096]{0:T(1024)}, u32[]{:S(2)}) copy-start(f32[4096]{0:T(1024)} %param.16) | copy-start | bytes 49156
  143.0 10.2 %all-to-all-start.1 = ((bf16[4,12,4096]{2,1,0:T(8,128)(2,1)}), bf16[4,12,4096]{2,1,0:T(8,128)(2,1)S(1)}, u32[]{:S(2)}, u32[]{:S(2)}) async-start(bf16[4,12,4096]{2,1,0:T(8,128)(2,1)} %reshape.89), calls=%async_computation.2 | async-start | bytes 1048576 | tf_op jit(solution)/shard_map/all_to_all | solution.py:61
  146.6 30.6 %all-gather.5.cloned.1.call-start = ((), (), s32[]{:S(2)}) async-start(), calls=%async_computation.5 | async-start | bytes 1179648 | tf_op jit(solution)/shard_map/all_gather | solution.py:72
  154.8 30.0 %copy-start.2 = (bf16[16,4096]{1,0:T(8,128)(2,1)}, bf16[16,4096]{1,0:T(8,128)(2,1)S(1)}, u32[]{:S(2)}) copy-start(bf16[16,4096]{1,0:T(8,128)(2,1)S(1)} %get-tuple-element.10) | copy-start | bytes 393220
  178.9 5.2 %collective-permute-start = (bf16[128,256]{1,0:T(8,128)(2,1)S(1)}, bf16[128,256]{1,0:T(8,128)(2,1)S(1)}, u32[]{:S(2)}, u32[]{:S(2)}) collective-permute-start(bf16[128,256]{1,0:T(8,128)(2,1)S(1)} %convolution_convert_fusion.1), channel_id=1, source_target_pairs={{0,8},{8,16},{16,24},{24,0},{1,9},{9,17},{17,25},{25,1},{2,10},{10... | collective-permute-start | bytes 196616 | tf_op jit(solution)/shard_map/ppermute | solution.py:12
Sparse Core Ops, SparseCore 0:
  25.7 37.9 all-gather.2
  101.8 39.2 reduce-scatter.1
  155.7 21.4 all-gather.4
where the time goes:
time: 192 us; the launch traced here: 191 us
  waiting for transfers between devices  109 us (57%)
  matrix products  40.3 us (21%)
  between operations  13.9 us (7%)
  blocking collectives  13.5 us (7%)
  local copies, waits for them, and re-layouts  6.24 us (3%)
  starting transfers between devices  5.26 us (3%)
  other arithmetic  3.58 us (2%)
    reduce_scatter x1, waiting for transfers between devices, body(): lax.psum_scatter(jnp.dot(block_rows, down_weight, preferred_element_type=...  38.6 us
    all_gather x1, waiting for transfers between devices, body(): block_rows = lax.all_gather(inbound, 'mp', axis=0, tiled=True)  38 us
    dot_general x1, matrix products, body(): jnp.dot(block_rows, down_weight, preferred_element_type=jnp.float32)  25 us
    all_gather x1, waiting for transfers between devices, body(): lax.all_gather(attn_input, 'mp', axis=0, tiled=True)  21.7 us
    all_to_all x1, blocking collectives, body(): lax.all_to_all(buffer, 'section', split_axis=0, concat_axis=0, tiled=True)  13.5 us
    dot_general x1, matrix products, body(): jnp.dot(block_rows, gate_weight, preferred_element_type=jnp.float32)  12.9 us
    all_to_all x1, waiting for transfers between devices, body(): lax.all_to_all(results, 'section', split_axis=0, concat_axis=0, tiled=True)  6.54 us
  transfers between devices with their start and end apart: 5, of which 5 were waited for; matrix products, arithmetic and copies ran while one was open for 0% of the time, Pallas kernels for 0%

commit v1 on v0

--- a/solution.py
+++ b/solution.py
@@ -4,6 +4,18 @@
 from jax.sharding import PartitionSpec as P
 
 epsilon = 1e-05
+
+
+def gather_by_bits(array, axis, dim):
+    ways, here, step = (lax.axis_size(axis), lax.axis_index(axis), array.shape[dim])
+    line, have = (array, 1)
+    while have < ways:
+        line = jnp.concatenate(
+            [line, lax.ppermute(line, axis, [(d, (d - have) % ways) for d in range(ways)])],
+            axis=dim,
+        )
+        have = 2 * have
+    return jnp.roll(line, here * step, axis=dim)
 
 
 def shifted(value, axis, steps):
@@ -69,9 +81,7 @@
     stream_out = updated.astype(jnp.bfloat16)
     attn_input = normalize(stream_out, attn_gain).astype(jnp.bfloat16)
     kv_local = jnp.dot(
-        lax.all_gather(attn_input, "mp", axis=0, tiled=True),
-        w_kv,
-        preferred_element_type=jnp.float32,
+        gather_by_bits(attn_input, "mp", 0), w_kv, preferred_element_type=jnp.float32
     ).astype(jnp.bfloat16)
     kv_decode = shifted(kv_local, "section", 1)
     return (stream_out, kv_decode)

time: 192 us -> 212 us (1.10)
  waiting for transfers between devices: 109 us -> 120 us
  local copies, waits for them, and re-layouts: 6.24 us -> 11.3 us
  starting transfers between devices: 5.26 us -> 7.84 us
    ppermute x0 -> x3, waiting for transfers between devices: none -> 33.5 us  [gather_by_bits(): lax.ppermute(line, axis, [(d, (d - have) % ways) for d in range(ways)])]
    all_gather x1 -> x0, waiting for transfers between devices: 21.7 us -> none  [body(): lax.all_gather(attn_input, 'mp', axis=0, tiled=True)]
    unnamed x14 -> x20, local copies, waits for them, and re-layouts: 2.28 us -> 6.54 us
    ppermute x0 -> x3, starting transfers between devices: none -> 2.64 us  [gather_by_bits(): lax.ppermute(line, axis, [(d, (d - have) % ways) for d in range(ways)])]
  transfers between devices with their start and end apart: 5 -> 7, of which waited for: 5 -> 7; matrix products, arithmetic and copies ran while one was open for 0% -> 1% of each run, Pallas kernels for 0% -> 0%
where the time goes in v1:
time: 212 us; the launch traced here: 211 us
  waiting for transfers between devices  120 us (57%)
  matrix products  40.3 us (19%)
  between operations  14.2 us (7%)
  blocking collectives  13.5 us (6%)
  local copies, waits for them, and re-layouts  11.3 us (5%)
  starting transfers between devices  7.84 us (4%)
  other arithmetic  3.64 us (2%)
    reduce_scatter x1, waiting for transfers between devices, body(): lax.psum_scatter(jnp.dot(block_rows, down_weight, preferred_element_type=...  38.6 us
    all_gather x1, waiting for transfers between devices, body(): block_rows = lax.all_gather(inbound, 'mp', axis=0, tiled=True)  38 us
    ppermute x3, waiting for transfers between devices, gather_by_bits(): lax.ppermute(line, axis, [(d, (d - have) % ways) for d in range(ways)])  33.5 us
    dot_general x1, matrix products, body(): jnp.dot(block_rows, down_weight, preferred_element_type=jnp.float32)  25.1 us
    all_to_all x1, blocking collectives, body(): lax.all_to_all(buffer, 'section', split_axis=0, concat_axis=0, tiled=True)  13.5 us
    dot_general x1, matrix products, body(): jnp.dot(block_rows, gate_weight, preferred_element_type=jnp.float32)  12.9 us
    unnamed x20, local copies, waits for them, and re-layouts  6.54 us
    all_to_all x1, waiting for transfers between devices, body(): lax.all_to_all(results, 'section', split_axis=0, concat_axis=0, tiled=True)  6.52 us
  transfers between devices with their start and end apart: 7, of which 7 were waited for; matrix products, arithmetic and copies ran while one was open for 1% of the time, Pallas kernels for 0%

profile of v1, /device:TPU:0, one launch (start us, length us, event | category | flops | bytes accessed | tf_op | source)
XLA Modules:
  0.0 211.2 jit_solution(14694533711070442002)
XLA Ops:
  7.2 0.0 copy-start
  7.2 0.0 all-gather.2.cloned.1.call-start
  7.2 0.9 copy.21
  8.1 0.1 eq.64
  8.2 0.1 fusion.31
  8.3 1.1 fusion.22
  9.4 0.1 reduce_window_sum.11
  9.4 0.2 select_reduce_fusion
  9.6 1.0 fusion.24
  10.6 0.2 broadcast_in_dim.16
  10.8 0.1 reshape.91
  10.9 0.3 convolution_convert_fusion
  11.2 13.5 %all_to_all.10 = bf16[4,12,4096]{2,1,0:T(8,128)(2,1)S(1)} all-to-all(bf16[4,12,4096]{2,1,0:T(8,128)(2,1)S(1)} %convolution_convert_fusion), channel_id=1, replica_groups=mesh['section'=4,'mp'=8] {'section'}, dimensions={0} | all-to-all | bytes 786432 | tf_op jit(solution)/shard_map/all_to_all | solution.py:56
  24.7 0.8 reshape.88
  25.6 0.0 all-gather.2.cloned.1.call-update
  25.6 0.0 reduce-scatter.2.cloned.1.call-start
  25.6 38.0 %all-gather.2.cloned.1.call-done = bf16[384,4096]{1,0:T(8,128)(2,1)} async-done(((bf16[48,4096]{1,0:T(8,128)(2,1)}), bf16[384,4096]{1,0:T(8,128)(2,1)}) %all-gather.2.cloned.1.call-update) | async-done | bytes 3145744 | tf_op jit(solution)/shard_map/all_gather | solution.py:61
  63.7 12.9 %fusion.4 = f32[384,1792]{1,0:T(8,128)} fusion(bf16[384,4096]{1,0:T(8,128)(2,1)} %all-gather.2.cloned.1.call-done, bf16[1,4096,1792]{2,1,0:T(8,128)(2,1)} %param.13), kind=kOutput, calls=%fused_computation.4 | convolution fusion | flops 5637144576 | bytes 20578304 | tf_op jit(solution)/shard_map/dot_general | solution.py:62
  76.6 25.1 %fusion.6 = bf16[384,4096]{1,0:T(8,128)(2,1)} fusion(bf16[1,1792,4096]{2,1,0:T(8,128)(2,1)} %param.15, bf16[384,4096]{1,0:T(8,128)(2,1)} %all-gather.2.cloned.1.call-done, bf16[1,4096,1792]{2,1,0:T(8,128)(2,1)} %param.14, f32[384,1792]{1,0:T(8,128)} %fusion.4), kind=kOutput, calls=%fused_computation.6 | convolution fusion | flops 11279990784 | bytes 38404096 | tf_op jit(solution)/shard_map/dot_general | solution.py:67
  101.6 0.0 copy-start.5
  101.6 0.0 copy-start.4
  101.6 0.0 reduce-scatter.2.cloned.1.call-update
  101.7 0.7 copy-done.5
  102.4 0.0 copy-start.1
  102.4 0.1 fusion.41
  102.5 0.0 copy-start.3
  102.5 38.6 %reduce-scatter.2.cloned.1.call-done = bf16[48,4096]{1,0:T(8,128)(2,1)} async-done(((bf16[384,4096]{1,0:T(8,128)(2,1)}), bf16[48,4096]{1,0:T(8,128)(2,1)}) %reduce-scatter.2.cloned.1.call-update) | async-done | bytes 393232 | tf_op jit(solution)/shard_map/reduce_scatter | solution.py:66
  141.1 1.9 reshape.89
  143.0 3.6 %all-to-all-start.1 = ((bf16[4,12,4096]{2,1,0:T(8,128)(2,1)}), bf16[4,12,4096]{2,1,0:T(8,128)(2,1)S(1)}, u32[]{:S(2)}, u32[]{:S(2)}) async-start(bf16[4,12,4096]{2,1,0:T(8,128)(2,1)} %reshape.89), calls=%async_computation.2 | async-start | bytes 1048576 | tf_op jit(solution)/shard_map/all_to_all | solution.py:73
  146.7 0.0 copy-done.4
  146.7 6.5 %all-to-all-done.1 = bf16[4,12,4096]{2,1,0:T(8,128)(2,1)S(1)} async-done(((bf16[4,12,4096]{2,1,0:T(8,128)(2,1)}), bf16[4,12,4096]{2,1,0:T(8,128)(2,1)S(1)}, u32[]{:S(2)}, u32[]{:S(2)}) %all-to-all-start.1) | async-done | bytes 393248 | tf_op jit(solution)/shard_map/all_to_all | solution.py:73
  153.2 0.3 convolution_bitcast_fusion
  153.5 0.3 reshape.90
  153.8 0.6 fusion.40
  154.4 0.0 copy-done.1
  154.4 0.4 fusion.19
  154.8 0.0 copy-start.2
  154.8 0.0 copy-done.3
  154.8 0.8 constant_dynamic-update-slice_fusion.7
  155.6 2.5 %collective-permute-start = (bf16[16,4096]{1,0:T(8,128)(2,1)S(1)}, bf16[16,4096]{1,0:T(8,128)(2,1)S(1)}, u32[]{:S(2)}, u32[]{:S(2)}) collective-permute-start(bf16[16,4096]{1,0:T(8,128)(2,1)S(1)} %get-tuple-element.3), channel_id=1, source_target_pairs={{0,7},{1,0},{2,1},{3,2},{4,3},{5,4},{6,5},{7,6},{8,15},{9,8},{10,9... | collective-permute-start | bytes 393224 | tf_op jit(solution)/shard_map/ppermute | solution.py:14
  158.1 2.5 %collective-permute-done = bf16[16,4096]{1,0:T(8,128)(2,1)S(1)} collective-permute-done((bf16[16,4096]{1,0:T(8,128)(2,1)S(1)}, bf16[16,4096]{1,0:T(8,128)(2,1)S(1)}, u32[]{:S(2)}, u32[]{:S(2)}) %collective-permute-start) | collective-permute-done | bytes 131104 | tf_op jit(solution)/shard_map/ppermute | solution.py:14
  160.6 0.1 collective-permute-start.1
  160.7 6.4 %collective-permute-done.1 = bf16[32,4096]{1,0:T(8,128)(2,1)S(1)} collective-permute-done((bf16[32,4096]{1,0:T(8,128)(2,1)S(1)}, bf16[32,4096]{1,0:T(8,128)(2,1)S(1)}, u32[]{:S(2)}, u32[]{:S(2)}) %collective-permute-start.1) | collective-permute-done | bytes 262176 | tf_op jit(solution)/shard_map/ppermute | solution.py:14
  167.2 0.1 collective-permute-start.2
  167.2 0.7 constant_dynamic-update-slice_fusion.6
  167.9 0.7 constant_dynamic-update-slice_fusion.5
  168.6 24.5 %collective-permute-done.2 = bf16[64,4096]{1,0:T(8,128)(2,1)S(1)} collective-permute-done((bf16[64,4096]{1,0:T(8,128)(2,1)S(1)}, bf16[64,4096]{1,0:T(8,128)(2,1)S(1)}, u32[]{:S(2)}, u32[]{:S(2)}) %collective-permute-start.2) | collective-permute-done | bytes 524320 | tf_op jit(solution)/shard_map/ppermute | solution.py:14
  193.1 0.8 constant_dynamic-update-slice_fusion.4
  194.0 0.7 constant_dynamic-update-slice_fusion.3
  194.6 0.7 constant_dynamic-update-slice_fusion.2
  195.3 0.7 constant_dynamic-update-slice_fusion.1
  196.0 0.8 constant_dynamic-update-slice_fusion
  196.8 0.0 copy-done.2
  196.8 0.0 copy-done
  196.9 1.7 convolution_convert_fusion.1
  198.5 1.5 collective-permute-start.3
  200.0 3.7 %collective-permute-done.3 = bf16[128,256]{1,0:T(8,128)(2,1)S(1)} collective-permute-done((bf16[128,256]{1,0:T(8,128)(2,1)S(1)}, bf16[128,256]{1,0:T(8,128)(2,1)S(1)}, u32[]{:S(2)}, u32[]{:S(2)}) %collective-permute-start.3) | collective-permute-done | bytes 65568 | tf_op jit(solution)/shard_map/ppermute | solution.py:24
  203.7 0.6 copy.46
  (8 shorter events, 0.1 us)
Async XLA Ops:
  7.2 189.7 %copy-start = (bf16[4096,256]{1,0:T(8,128)(2,1)S(1)}, bf16[4096,256]{1,0:T(8,128)(2,1)}, u32[]{:S(2)}) copy-start(bf16[4096,256]{1,0:T(8,128)(2,1)} %param.17) | copy-start | bytes 6291460
  7.2 56.5 %all-gather.2.cloned.1.call-start = ((), (), s32[]{:S(2)}) async-start(), calls=%async_computation.3 | async-start | bytes 3538944 | tf_op jit(solution)/shard_map/all_gather | solution.py:61
  25.6 115.5 %reduce-scatter.2.cloned.1.call-start = ((), (), s32[]{:S(2)}) async-start(), calls=%async_computation.4 | async-start | bytes 3538944 | tf_op jit(solution)/shard_map/reduce_scatter | solution.py:66
  101.6 0.8 copy-start.5
  101.6 45.0 %copy-start.4 = (s32[16,2]{0,1:T(2,128)S(1)}, s32[16,2]{0,1:T(2,128)}, u32[]{:S(2)}) copy-start(s32[16,2]{0,1:T(2,128)} %param.12) | copy-start | bytes 388
  102.4 52.0 %copy-start.1 = (bf16[16,4096]{1,0:T(8,128)(2,1)S(1)}, bf16[16,4096]{1,0:T(8,128)(2,1)}, u32[]{:S(2)}) copy-start(bf16[16,4096]{1,0:T(8,128)(2,1)} %param.9) | copy-start | bytes 393220
  102.5 52.3 %copy-start.3 = (f32[4096]{0:T(1024)S(1)}, f32[4096]{0:T(1024)}, u32[]{:S(2)}) copy-start(f32[4096]{0:T(1024)} %param.16) | copy-start | bytes 49156
  143.0 10.2 %all-to-all-start.1 = ((bf16[4,12,4096]{2,1,0:T(8,128)(2,1)}), bf16[4,12,4096]{2,1,0:T(8,128)(2,1)S(1)}, u32[]{:S(2)}, u32[]{:S(2)}) async-start(bf16[4,12,4096]{2,1,0:T(8,128)(2,1)} %reshape.89), calls=%async_computation.2 | async-start | bytes 1048576 | tf_op jit(solution)/shard_map/all_to_all | solution.py:73
  154.8 42.1 %copy-start.2 = (bf16[16,4096]{1,0:T(8,128)(2,1)}, bf16[16,4096]{1,0:T(8,128)(2,1)S(1)}, u32[]{:S(2)}) copy-start(bf16[16,4096]{1,0:T(8,128)(2,1)S(1)} %get-tuple-element.12) | copy-start | bytes 393220
  155.6 5.0 %collective-permute-start = (bf16[16,4096]{1,0:T(8,128)(2,1)S(1)}, bf16[16,4096]{1,0:T(8,128)(2,1)S(1)}, u32[]{:S(2)}, u32[]{:S(2)}) collective-permute-start(bf16[16,4096]{1,0:T(8,128)(2,1)S(1)} %get-tuple-element.3), channel_id=1, source_target_pairs={{0,7},{1,0},{2,1},{3,2},{4,3},{5,4},{6,5},{7,6},{8,15},{9,8},{10,9... | collective-permute-start | bytes 393224 | tf_op jit(solution)/shard_map/ppermute | solution.py:14
  160.6 6.5 %collective-permute-start.1 = (bf16[32,4096]{1,0:T(8,128)(2,1)S(1)}, bf16[32,4096]{1,0:T(8,128)(2,1)S(1)}, u32[]{:S(2)}, u32[]{:S(2)}) collective-permute-start(bf16[32,4096]{1,0:T(8,128)(2,1)S(1)} %pad_maximum_fusion.1), channel_id=1, source_target_pairs={{0,6},{1,7},{2,0},{3,1},{4,2},{5,3},{6,4},{7,5},{8,14},{9,15},{10,... | collective-permute-start | bytes 786440 | tf_op jit(solution)/shard_map/ppermute | solution.py:14
  167.2 26.0 %collective-permute-start.2 = (bf16[64,4096]{1,0:T(8,128)(2,1)S(1)}, bf16[64,4096]{1,0:T(8,128)(2,1)S(1)}, u32[]{:S(2)}, u32[]{:S(2)}) collective-permute-start(bf16[64,4096]{1,0:T(8,128)(2,1)S(1)} %pad_maximum_fusion), channel_id=1, source_target_pairs={{0,4},{1,5},{2,6},{3,7},{4,0},{5,1},{6,2},{7,3},{8,12},{9,13},{10,... | collective-permute-start | bytes 1572872 | tf_op jit(solution)/shard_map/ppermute | solution.py:14
  198.5 5.2 %collective-permute-start.3 = (bf16[128,256]{1,0:T(8,128)(2,1)S(1)}, bf16[128,256]{1,0:T(8,128)(2,1)S(1)}, u32[]{:S(2)}, u32[]{:S(2)}) collective-permute-start(bf16[128,256]{1,0:T(8,128)(2,1)S(1)} %convolution_convert_fusion.1), channel_id=1, source_target_pairs={{0,8},{8,16},{16,24},{24,0},{1,9},{9,17},{17,25},{25,1},{2,10},{10... | collective-permute-start | bytes 196616 | tf_op jit(solution)/shard_map/ppermute | solution.py:24
Sparse Core Ops, SparseCore 0:
  25.7 37.9 all-gather.1
  101.8 39.2 reduce-scatter.1
